TPU v7x, 32 devices: a whole 2x2x4 slice. The times are simulated.
32 devices in a mesh: prow: 4 (over x, core), pcol: 8 (over z, y).
Axes of the slice: x: 2, y: 2, z: 4, core: 2. Of those that a mesh axis runs over, the one named last changes fastest.
Arguments:
- panels: bfloat16 [2, 48, 2048, 256], P(None, 'pcol', 'prow'), may hold values from -0.59765625 to 0.59765625
- inverses: bfloat16 [2, 48, 256, 256], P(None, 'pcol', 'prow'), may hold values from -0.25 to 0.25
- dest: int32 [48, 8, 8], P('pcol', 'prow'), may hold values from 0 to 7, as said below
- target: int32 [48, 8, 8], P('pcol', 'prow'), may hold values from 0 to 1
- ancestors: float32 [2, 2048, 2048], P(None, 'prow', 'pcol'), may hold values from -6 to 6
Outputs:
- factor: bfloat16 [2, 48, 2048, 256], P(None, 'pcol', 'prow')
- schur: float32 [2, 2048, 2048], P(None, 'prow', 'pcol')
Inputs may be any that keep to these rules, and one draw needn't show every extreme that they name: `dest`: among the 96 update blocks of one device (its leaves, its block rows), at most 24 name any one process column; on every process row one process column is named by exactly 24 blocks of every device of that row.
All inputs are finite; a program needn't handle non-finite values.
Results may differ from a plain program's by a relative error of at most 0.0045.
Values may be sent and summed in bfloat16 or wider, within the bound.
No kernel may reach another device: no remote copies, remote signals or barrier semaphores. Data moves between devices by JAX's collectives and lax.ppermute only.
A program may use at most 128 MiB of HBM per device.

v0:
```python
import jax
import jax.numpy as jnp
from jax import lax
from jax.sharding import PartitionSpec as P


def complex_product(left_real, left_imag, right_real, right_imag, pattern):

    def single(first_operand, second):
        return jnp.einsum(pattern, first_operand, second, preferred_element_type=jnp.float32)

    real_part = single(left_real, right_real) - single(left_imag, right_imag)
    imag_part = single(left_real, right_imag) + single(left_imag, right_real)
    return jnp.stack([real_part, imag_part]).astype(jnp.bfloat16)


def local(panels, inverses, dest, target, ancestors):
    inverse_full = lax.all_gather(inverses, "prow", axis=2, tiled=True)
    lower_panel = complex_product(
        panels[0], panels[1], inverse_full[0], inverse_full[1], "lrk,lkc->lrc"
    )
    segment = lax.all_gather(panels, "prow", axis=2, tiled=True)
    update = complex_product(lower_panel[0], lower_panel[1], segment[0], segment[1], "lrk,lck->lrc")
    block_width = panels.shape[3]
    leaf_count = panels.shape[1]
    local_rows = panels.shape[2] // block_width
    front_blocks = update.shape[3] // block_width
    blocks = update.reshape(2, leaf_count, local_rows, block_width, front_blocks, block_width)
    blocks = blocks.transpose(1, 2, 4, 0, 3, 5).reshape(-1, 2, block_width, block_width)
    block_count = blocks.shape[0]
    column_count = lax.axis_size("pcol")
    owned_blocks = ancestors.shape[1] // block_width
    dest_flat = dest.reshape(-1)
    target_flat = target.reshape(-1)
    slot_keys = dest_flat * owned_blocks + target_flat
    select = (
        jnp.arange(column_count * owned_blocks, dtype=jnp.int32)[:, None] == slot_keys[None, :]
    ).astype(jnp.bfloat16)
    merged = jnp.dot(select, blocks.reshape(block_count, -1), preferred_element_type=jnp.float32)
    arrived = lax.all_to_all(
        merged.astype(jnp.bfloat16), "pcol", split_axis=0, concat_axis=0, tiled=True
    ).astype(merged.dtype)
    summed = jnp.sum(arrived.reshape(column_count, owned_blocks, -1), axis=0)
    summed = summed.reshape(owned_blocks, 2, block_width, block_width).transpose(1, 0, 2, 3)
    summed = summed.reshape(2, owned_blocks * block_width, block_width)
    return (lower_panel, ancestors - summed)


def solution(mesh):
    return jax.shard_map(
        local,
        mesh=mesh,
        in_specs=(
            P(None, "pcol", "prow", None),
            P(None, "pcol", "prow", None),
            P("pcol", "prow", None),
            P("pcol", "prow", None),
            P(None, "prow", "pcol"),
        ),
        out_specs=(P(None, "pcol", "prow", None), P(None, "prow", "pcol")),
        check_vma=False,
    )
```

profile of v0, /device:TPU:0, one launch (start us, length us, event | category | flops | bytes accessed | tf_op | source)
XLA Modules:
  0.0 374.9 jit_solution(875081187153657765)
XLA Ops:
  7.2 0.0 copy-start
  7.2 0.0 copy-start.5
  7.2 0.0 copy-start.4
  7.2 0.0 all-gather.3.cloned.1.call-start
  7.2 0.7 all-gather.3.cloned.1.call-update
  7.9 0.0 all-gather.5.cloned.1.call-start
  8.0 0.7 all-gather.5.cloned.1.call-update
  8.7 0.0 copy-done.5
  8.7 0.0 copy-done.4
  8.7 0.1 add.18
  8.8 23.1 %all-gather.3.cloned.1.call-done = bf16[2,6,256,256]{3,2,1,0:T(8,128)(2,1)} async-done(((bf16[2,6,64,256]{3,2,1,0:T(8,128)(2,1)}), bf16[2,6,256,256]{3,2,1,0:T(8,128)(2,1)}) %all-gather.3.cloned.1.call-update) | async-done | bytes 1572880 | tf_op jit(solution)/shard_map/all_gather | solution.py:18
  32.0 0.0 copy-done
  32.0 0.0 copy-start.2
  32.0 1.8 fusion.6
  33.8 0.0 copy-done.2
  33.8 0.0 copy-start.1
  33.8 0.6 fusion.4
  34.4 1.3 copy-done.1
  35.7 0.6 subtract_convert_fusion.1
  36.3 0.6 add_convert_fusion.1
  36.8 78.8 %all-gather.5.cloned.1.call-done = bf16[2,6,2048,256]{3,2,1,0:T(8,128)(2,1)} async-done(((bf16[2,6,512,256]{3,2,1,0:T(8,128)(2,1)}), bf16[2,6,2048,256]{3,2,1,0:T(8,128)(2,1)}) %all-gather.5.cloned.1.call-update) | async-done | bytes 12582928 | tf_op jit(solution)/shard_map/all_gather | solution.py:22
  115.6 12.9 %fusion.1 = f32[6,512,2048]{2,1,0:T(8,128)} fusion(bf16[6,512,256]{2,1,0:T(8,128)(2,1)S(1)} %subtract_convert_fusion.1, bf16[2,6,2048,256]{3,2,1,0:T(8,128)(2,1)} %all-gather.5.cloned.1.call-done), kind=kOutput, calls=%fused_computation.8 | convolution fusion | flops 3221225472 | bytes 33030144 | tf_op jit(solution)/shard_map/lrk,lck->lrc/dot_general | solution.py:10
  128.5 18.0 %add_convert_fusion = bf16[6,512,2048]{2,1,0:T(8,128)(2,1)} fusion(f32[6,512,2048]{2,1,0:T(8,128)} %fusion.1, bf16[6,512,256]{2,1,0:T(8,128)(2,1)S(1)} %add_convert_fusion.1, bf16[2,6,2048,256]{3,2,1,0:T(8,128)(2,1)} %all-gather.5.cloned.1.call-done), kind=kOutput, calls=%fused_computation.2 | convolution fusion | flops 3233808384 | bytes 45613056 | tf_op jit(solution)/shard_map/lrk,lck->lrc/dot_general | solution.py:10
  146.5 8.3 %copy.13 = bf16[384,8,8,256]{3,2,1,0:T(8,128)(2,1)S(1)} copy(bf16[384,8,8,256]{3,1,2,0:T(8,128)(2,1)} %bitcast.53) | data formatting | bytes 25165824
  154.8 6.0 %copy.10 = bf16[1,6,2,256,8,256]{5,3,0,4,2,1:T(8,128)(2,1)} copy(bf16[1,6,2,256,8,256]{5,4,3,2,1,0:T(8,128)(2,1)S(1)} %bitcast.54) | data formatting | bytes 25165824 | tf_op jit(solution)/shard_map/stack | solution.py:14
  160.8 12.9 %fusion = f32[6,512,2048]{2,1,0:T(8,128)} fusion(bf16[6,512,256]{2,1,0:T(8,128)(2,1)S(1)} %subtract_convert_fusion.1, bf16[2,6,2048,256]{3,2,1,0:T(8,128)(2,1)} %all-gather.5.cloned.1.call-done), kind=kOutput, calls=%fused_computation.7 | convolution fusion | flops 3221225472 | bytes 33030144 | tf_op jit(solution)/shard_map/lrk,lck->lrc/dot_general | solution.py:10
  173.7 18.1 %subtract_convert_fusion = bf16[6,512,2048]{2,1,0:T(8,128)(2,1)} fusion(f32[6,512,2048]{2,1,0:T(8,128)} %fusion, bf16[6,512,256]{2,1,0:T(8,128)(2,1)S(1)} %add_convert_fusion.1, bf16[2,6,2048,256]{3,2,1,0:T(8,128)(2,1)} %all-gather.5.cloned.1.call-done), kind=kOutput, calls=%fused_computation.3 | convolution fusion | flops 3233808384 | bytes 45613056 | tf_op jit(solution)/shard_map/lrk,lck->lrc/dot_general | solution.py:10
  191.7 0.0 slice-start
  191.7 0.0 slice-start.1
  191.7 9.6 %copy.12 = bf16[384,8,8,256]{3,2,1,0:T(8,128)(2,1)S(1)} copy(bf16[384,8,8,256]{3,1,2,0:T(8,128)(2,1)} %bitcast.52) | data formatting | bytes 25165824
  201.4 0.0 slice-start.2
  201.4 6.2 %copy.9 = bf16[1,6,2,256,8,256]{5,3,0,4,2,1:T(8,128)(2,1)S(1)} copy(bf16[1,6,2,256,8,256]{5,4,3,2,1,0:T(8,128)(2,1)S(1)} %bitcast.55) | data formatting | bytes 25165824 | tf_op jit(solution)/shard_map/stack | solution.py:14
  207.6 0.0 slice-done
  207.6 0.0 slice-done.1
  207.6 0.0 slice-done.2
  207.6 10.0 %maximum_bitcast_fusion = bf16[6,2,8,2,256,256]{5,4,3,2,1,0:T(8,128)(2,1)} fusion(bf16[1,6,2,256,8,256]{5,3,0,4,2,1:T(8,128)(2,1)S(1)} %bitcast.57, bf16[1,6,2,256,8,256]{5,3,0,4,2,1:T(8,128)(2,1)S(1)} %copy.9), kind=kLoop, calls=%fused_computation.1 | loop fusion | flops 12582912 | bytes 50331648 | tf_op jit(solution)/shard_map/transpose | solution.py:29
  217.6 25.1 %reshape_reshape.3 = bf16[96,131072]{1,0:T(8,128)(2,1)} reshape(bf16[6,2,8,2,256,256]{5,4,3,2,1,0:T(8,128)(2,1)} %maximum_bitcast_fusion) | data formatting | bytes 50331648 | tf_op jit(solution)/shard_map/reshape;reshape | solution.py:39
  242.7 12.0 %convolution_convert_fusion = bf16[16,131072]{1,0:T(8,128)(2,1)} fusion(bf16[96,131072]{1,0:T(8,128)(2,1)} %reshape_reshape.3, s32[96]{0:T(128)S(1)} %add.18), kind=kOutput, calls=%fused_computation | convolution fusion | flops 404751872 | bytes 29360512 | tf_op jit(solution)/shard_map/dot_general | solution.py:39
  254.7 5.5 %all_to_all.6 = bf16[8,2,131072]{2,1,0:T(2,128)(2,1)} reshape(bf16[16,131072]{1,0:T(8,128)(2,1)} %convolution_convert_fusion) | data formatting | bytes 8388608 | tf_op jit(solution)/shard_map/all_to_all | solution.py:40
  260.2 5.5 %all-to-all-start = ((bf16[8,2,131072]{2,1,0:T(2,128)(2,1)}), bf16[8,2,131072]{2,1,0:T(2,128)(2,1)}, u32[]{:S(2)}, u32[]{:S(2)}) async-start(bf16[8,2,131072]{2,1,0:T(2,128)(2,1)} %all_to_all.6), calls=%async_computation | async-start | bytes 8388608 | tf_op jit(solution)/shard_map/all_to_all | solution.py:40
  265.7 1.9 pad_maximum_fusion
  267.7 91.8 %all-to-all-done = bf16[8,2,131072]{2,1,0:T(2,128)(2,1)} async-done(((bf16[8,2,131072]{2,1,0:T(2,128)(2,1)}), bf16[8,2,131072]{2,1,0:T(2,128)(2,1)}, u32[]{:S(2)}, u32[]{:S(2)}) %all-to-all-start) | async-done | bytes 4194336 | tf_op jit(solution)/shard_map/all_to_all | solution.py:40
  359.4 6.3 %convert_reduce_fusion = f32[2,131072]{1,0:T(2,128)S(1)} fusion(bf16[8,2,131072]{2,1,0:T(2,128)(2,1)} %all-to-all-done), kind=kLoop, calls=%fused_computation.4 | loop fusion | flops 3932160 | bytes 5242880 | tf_op jit(solution)/shard_map/reduce_sum | solution.py:43
  365.7 0.0 copy-start.3
  365.8 0.1 copy.14
  365.8 0.1 copy.11
  365.9 1.1 copy-done.3
  367.0 1.1 bitcast_subtract_fusion
  (2 shorter events, 0.0 us)
Async XLA Ops:
  7.2 24.8 %copy-start = (bf16[2,6,512,256]{3,2,1,0:T(8,128)(2,1)S(1)}, bf16[2,6,512,256]{3,2,1,0:T(8,128)(2,1)}, u32[]{:S(2)}) copy-start(bf16[2,6,512,256]{3,2,1,0:T(8,128)(2,1)} %param.5) | copy-start | bytes 9437188
  7.2 1.5 copy-start.5
  7.2 1.5 copy-start.4
  7.2 24.8 %all-gather.3.cloned.1.call-start = ((), (), s32[]{:S(2)}) async-start(), calls=%async_computation.1 | async-start | bytes 1966080 | tf_op jit(solution)/shard_map/all_gather | solution.py:18
  7.9 107.7 %all-gather.5.cloned.1.call-start = ((), (), s32[]{:S(2)}) async-start(), calls=%async_computation.2 | async-start | bytes 15728640 | tf_op jit(solution)/shard_map/all_gather | solution.py:22
  32.0 1.8 copy-start.2
  33.8 1.9 copy-start.1
  191.7 15.8 %slice-start = ((s8[12582912]{0:T(1024)(128)(4,1)}), s8[4194304]{0:T(1024)(128)(4,1)S(1)}, s32[]{:S(2)}) async-start(s8[12582912]{0:T(1024)(128)(4,1)} %bitcast.56), calls=%async_computation.3 | async-start | bytes 8388608
  191.7 15.8 %slice-start.1 = ((s8[12582912]{0:T(1024)(128)(4,1)}), s8[4194304]{0:T(1024)(128)(4,1)S(1)}, s32[]{:S(2)}) async-start(s8[12582912]{0:T(1024)(128)(4,1)} %bitcast.56), calls=%async_computation.4 | async-start | bytes 8388608
  201.4 6.2 %slice-start.2 = ((s8[12582912]{0:T(1024)(128)(4,1)}), s8[4194304]{0:T(1024)(128)(4,1)S(1)}, s32[]{:S(2)}) async-start(s8[12582912]{0:T(1024)(128)(4,1)} %bitcast.56), calls=%async_computation.5 | async-start | bytes 8388608
  260.2 99.2 %all-to-all-start = ((bf16[8,2,131072]{2,1,0:T(2,128)(2,1)}), bf16[8,2,131072]{2,1,0:T(2,128)(2,1)}, u32[]{:S(2)}, u32[]{:S(2)}) async-start(bf16[8,2,131072]{2,1,0:T(2,128)(2,1)} %all_to_all.6), calls=%async_computation | async-start | bytes 8388608 | tf_op jit(solution)/shard_map/all_to_all | solution.py:40
  365.7 1.2 copy-start.3
Sparse Core Ops, SparseCore 0:
  9.6 22.3 all-gather.2
  33.5 82.0 all-gather.4
where the time goes:
time: 376 us; the launch traced here: 375 us
  waiting for transfers between devices  195 us (52%)
  matrix products  77.3 us (21%)
  local copies, waits for them, and re-layouts  63.4 us (17%)
  other arithmetic  19.3 us (5%)
  between operations  14.2 us (4%)
  starting transfers between devices  5.59 us (1%)
    all_to_all x1, waiting for transfers between devices, local(): lax.all_to_all(merged.astype(jnp.bfloat16), 'pcol', split_axis=0, concat_...  91.8 us
    all_gather x1, waiting for transfers between devices, local(): segment = lax.all_gather(panels, 'prow', axis=2, tiled=True)  78.8 us
    dot_general x8, matrix products, single(): jnp.einsum(pattern, first_operand, second, preferred_element_type=jnp.flo...  65.3 us
    another operation x1, local copies, waits for them, and re-layouts, local(): blocks.reshape(block_count, -1)  25.1 us
    all_gather x1, waiting for transfers between devices, local(): inverse_full = lax.all_gather(inverses, 'prow', axis=2, tiled=True)  23.1 us
    unnamed x21, local copies, waits for them, and re-layouts  20.4 us
    another operation x2, local copies, waits for them, and re-layouts, complex_product(): return jnp.stack([real_part, imag_part]).astype(jnp.bfloat16)  12.2 us
    dot_general x1, matrix products, local(): jnp.dot(select, blocks.reshape(block_count, -1), preferred_element_type=j...  12 us
  transfers between devices with their start and end apart: 3, of which 3 were waited for; matrix products, arithmetic and copies ran while one was open for 1% of the time, Pallas kernels for 0%

commit v1 on v0

--- a/solution.py
+++ b/solution.py
@@ -2,6 +2,7 @@
 import jax.numpy as jnp
 from jax import lax
 from jax.sharding import PartitionSpec as P
+from jax.lax import axis_index, axis_size, ppermute
 
 
 def complex_product(left_real, left_imag, right_real, right_imag, pattern):
@@ -19,7 +20,16 @@
     lower_panel = complex_product(
         panels[0], panels[1], inverse_full[0], inverse_full[1], "lrk,lkc->lrc"
     )
-    segment = lax.all_gather(panels, "prow", axis=2, tiled=True)
+    w_next = axis_index("prow")
+    high = axis_size("prow")
+    state_now, s_next = (high, w_next)
+    segment, q_next = (panels, 1)
+    while q_next < state_now:
+        new = ppermute(segment, "prow", [(j, j ^ q_next) for j in range(state_now)])
+        field_out = jnp.concatenate([segment, new], axis=2)
+        known = jnp.concatenate([new, segment], axis=2)
+        segment = jnp.where(s_next & q_next == 0, field_out, known)
+        q_next = 2 * q_next
     update = complex_product(lower_panel[0], lower_panel[1], segment[0], segment[1], "lrk,lck->lrc")
     block_width = panels.shape[3]
     leaf_count = panels.shape[1]

time: 376 us -> 443 us (1.18)
  waiting for transfers between devices: 195 us -> 236 us
  other arithmetic: 19.3 us -> 43.1 us
    ppermute x0 -> x2, waiting for transfers between devices: none -> 117 us  [local(): new = ppermute(segment, 'prow', [(j, j ^ q_next) for j in range(state_now)])]
    all_gather x1 -> x0, waiting for transfers between devices: 78.8 us -> none  [local(): segment = lax.all_gather(panels, 'prow', axis=2, tiled=True)]
    select_n x0 -> x2, other arithmetic: none -> 23.8 us  [local(): segment = jnp.where(s_next & q_next == 0, field_out, known)]
    all_gather x1, waiting for transfers between devices: 23.1 us -> 28.5 us  [local(): inverse_full = lax.all_gather(inverses, 'prow', axis=2, tiled=True)]
  transfers between devices with their start and end apart: 3 -> 4, of which waited for: 3 -> 4; matrix products, arithmetic and copies ran while one was open for 1% -> 2% of each run, Pallas kernels for 0% -> 0%
where the time goes in v1:
time: 443 us
  waiting for transfers between devices  236 us (53%)
  matrix products  78.5 us (18%)
  local copies, waits for them, and re-layouts  61.2 us (14%)
  other arithmetic  43.1 us (10%)
  between operations  14.2 us (3%)
  starting transfers between devices  9.53 us (2%)
    ppermute x2, waiting for transfers between devices, local(): new = ppermute(segment, 'prow', [(j, j ^ q_next) for j in range(state_now)])  117 us
    all_to_all x1, waiting for transfers between devices, local(): lax.all_to_all(merged.astype(jnp.bfloat16), 'pcol', split_axis=0, concat_...  90.8 us
    dot_general x8, matrix products, single(): jnp.einsum(pattern, first_operand, second, preferred_element_type=jnp.flo...  66.5 us
    all_gather x1, waiting for transfers between devices, local(): inverse_full = lax.all_gather(inverses, 'prow', axis=2, tiled=True)  28.5 us
    another operation x1, local copies, waits for them, and re-layouts, local(): blocks.reshape(block_count, -1)  25.1 us
    select_n x2, other arithmetic, local(): segment = jnp.where(s_next & q_next == 0, field_out, known)  23.8 us
    unnamed x21, local copies, waits for them, and re-layouts  18.1 us
    another operation x2, local copies, waits for them, and re-layouts, complex_product(): return jnp.stack([real_part, imag_part]).astype(jnp.bfloat16)  12.3 us
  transfers between devices with their start and end apart: 4, of which 4 were waited for; matrix products, arithmetic and copies ran while one was open for 2% of the time, Pallas kernels for 0%

profile of v1, /device:TPU:0, one launch (start us, length us, event | category | flops | bytes accessed | tf_op | source)
XLA Modules:
  0.0 442.6 jit_solution(4905330703197903651)
XLA Ops:
  7.2 0.0 all-gather.2.cloned.1.call-start
  7.2 0.6 collective-permute-start
  7.8 0.0 copy-start.4
  7.8 0.0 copy-start.5
  7.8 0.0 copy-start
  7.8 5.6 %collective-permute-done = bf16[2,6,512,256]{3,2,1,0:T(8,128)(2,1)} collective-permute-done((bf16[2,6,512,256]{3,2,1,0:T(8,128)(2,1)}, bf16[2,6,512,256]{3,2,1,0:T(8,128)(2,1)}, u32[]{:S(2)}, u32[]{:S(2)}) %collective-permute-start) | collective-permute-done | bytes 3145760 | tf_op jit(solution)/shard_map/ppermute | solution.py:28
  13.4 8.6 %maximum_select_fusion.1 = bf16[2,6,1024,256]{3,2,1,0:T(8,128)(2,1)} fusion(bf16[2,6,512,256]{3,2,1,0:T(8,128)(2,1)} %collective-permute-done, bf16[2,6,512,256]{3,2,1,0:T(8,128)(2,1)} %param.5, pred[]{:T(512)S(6)} %eq.23), kind=kLoop, calls=%fused_computation.8 | loop fusion | flops 28311552 | bytes 12582913 | tf_op jit(solution)/shard_map/jit(_where)/select_n | solution.py:31
  22.0 2.8 collective-permute-start.1
  24.8 0.0 all-gather.2.cloned.1.call-update
  24.9 0.0 copy-done.4
  24.9 0.0 copy-done.5
  24.9 0.1 add.18
  25.0 28.5 %all-gather.2.cloned.1.call-done = bf16[2,6,256,256]{3,2,1,0:T(8,128)(2,1)} async-done(((bf16[2,6,64,256]{3,2,1,0:T(8,128)(2,1)}), bf16[2,6,256,256]{3,2,1,0:T(8,128)(2,1)}) %all-gather.2.cloned.1.call-update) | async-done | bytes 1572880 | tf_op jit(solution)/shard_map/all_gather | solution.py:19
  53.5 0.0 copy-done
  53.5 0.0 copy-start.1
  53.5 0.0 copy-start.2
  53.5 1.9 fusion.4
  55.3 1.7 fusion.6
  57.1 0.0 copy-done.1
  57.1 0.0 copy-done.2
  57.1 0.6 add_convert_fusion.1
  57.7 0.6 subtract_convert_fusion.1
  58.2 111.1 %collective-permute-done.1 = bf16[2,6,1024,256]{3,2,1,0:T(8,128)(2,1)} collective-permute-done((bf16[2,6,1024,256]{3,2,1,0:T(8,128)(2,1)}, bf16[2,6,1024,256]{3,2,1,0:T(8,128)(2,1)}, u32[]{:S(2)}, u32[]{:S(2)}) %collective-permute-start.1) | collective-permute-done | bytes 6291488 | tf_op jit(solution)/shard_map/ppermute | solution.py:28
  169.4 15.2 %maximum_select_fusion = bf16[2,6,2048,256]{3,2,1,0:T(8,128)(2,1)} fusion(bf16[2,6,1024,256]{3,2,1,0:T(8,128)(2,1)} %collective-permute-done.1, bf16[2,6,1024,256]{3,2,1,0:T(8,128)(2,1)} %maximum_select_fusion.1, pred[]{:T(512)S(6)} %eq.22), kind=kLoop, calls=%fused_computation.4 | loop fusion | flops 56623104 | bytes 25165824 | tf_op jit(solution)/shard_map/jit(_where)/select_n | solution.py:31
  184.6 12.8 %fusion.1 = f32[6,512,2048]{2,1,0:T(8,128)} fusion(bf16[6,512,256]{2,1,0:T(8,128)(2,1)S(1)} %add_convert_fusion.1, bf16[2,6,2048,256]{3,2,1,0:T(8,128)(2,1)} %maximum_select_fusion), kind=kOutput, calls=%fused_computation.10 | convolution fusion | flops 3221225472 | bytes 33030144 | tf_op jit(solution)/shard_map/lrk,lck->lrc/dot_general | solution.py:11
  197.5 12.9 %fusion = f32[6,512,2048]{2,1,0:T(8,128)} fusion(bf16[6,512,256]{2,1,0:T(8,128)(2,1)S(1)} %add_convert_fusion.1, bf16[2,6,2048,256]{3,2,1,0:T(8,128)(2,1)} %maximum_select_fusion), kind=kOutput, calls=%fused_computation.9 | convolution fusion | flops 3221225472 | bytes 33030144 | tf_op jit(solution)/shard_map/lrk,lck->lrc/dot_general | solution.py:11
  210.3 18.1 %subtract_convert_fusion = bf16[6,512,2048]{2,1,0:T(8,128)(2,1)} fusion(f32[6,512,2048]{2,1,0:T(8,128)} %fusion.1, bf16[6,512,256]{2,1,0:T(8,128)(2,1)S(1)} %subtract_convert_fusion.1, bf16[2,6,2048,256]{3,2,1,0:T(8,128)(2,1)} %maximum_select_fusion), kind=kOutput, calls=%fused_computation.3 | convolution fusion | flops 3233808384 | bytes 45613056 | tf_op jit(solution)/shard_map/lrk,lck->lrc/dot_general | solution.py:11
  228.4 8.3 %copy.12 = bf16[384,8,8,256]{3,2,1,0:T(8,128)(2,1)S(1)} copy(bf16[384,8,8,256]{3,1,2,0:T(8,128)(2,1)} %bitcast.53) | data formatting | bytes 25165824
  236.7 6.1 %copy.9 = bf16[1,6,2,256,8,256]{5,3,0,4,2,1:T(8,128)(2,1)} copy(bf16[1,6,2,256,8,256]{5,4,3,2,1,0:T(8,128)(2,1)S(1)} %bitcast.54) | data formatting | bytes 25165824 | tf_op jit(solution)/shard_map/stack | solution.py:15
  242.8 18.0 %add_convert_fusion = bf16[6,512,2048]{2,1,0:T(8,128)(2,1)} fusion(f32[6,512,2048]{2,1,0:T(8,128)} %fusion, bf16[6,512,256]{2,1,0:T(8,128)(2,1)S(1)} %subtract_convert_fusion.1, bf16[2,6,2048,256]{3,2,1,0:T(8,128)(2,1)} %maximum_select_fusion), kind=kOutput, calls=%fused_computation.2 | convolution fusion | flops 3233808384 | bytes 45613056 | tf_op jit(solution)/shard_map/lrk,lck->lrc/dot_general | solution.py:11
  260.8 0.0 slice-start
  260.8 0.0 slice-start.1
  260.8 9.6 %copy.13 = bf16[384,8,8,256]{3,2,1,0:T(8,128)(2,1)S(1)} copy(bf16[384,8,8,256]{3,1,2,0:T(8,128)(2,1)} %bitcast.52) | data formatting | bytes 25165824
  270.5 0.0 slice-start.2
  270.5 6.2 %copy.10 = bf16[1,6,2,256,8,256]{5,3,0,4,2,1:T(8,128)(2,1)S(1)} copy(bf16[1,6,2,256,8,256]{5,4,3,2,1,0:T(8,128)(2,1)S(1)} %bitcast.55) | data formatting | bytes 25165824 | tf_op jit(solution)/shard_map/stack | solution.py:15
  276.7 0.0 slice-done
  276.7 0.0 slice-done.1
  276.7 0.0 slice-done.2
  276.7 9.9 %maximum_bitcast_fusion = bf16[6,2,8,2,256,256]{5,4,3,2,1,0:T(8,128)(2,1)} fusion(bf16[1,6,2,256,8,256]{5,3,0,4,2,1:T(8,128)(2,1)S(1)} %copy.10, bf16[1,6,2,256,8,256]{5,3,0,4,2,1:T(8,128)(2,1)S(1)} %bitcast.57), kind=kLoop, calls=%fused_computation.1 | loop fusion | flops 12582912 | bytes 50331648 | tf_op jit(solution)/shard_map/transpose | solution.py:39
  286.6 25.1 %reshape_reshape.3 = bf16[96,131072]{1,0:T(8,128)(2,1)} reshape(bf16[6,2,8,2,256,256]{5,4,3,2,1,0:T(8,128)(2,1)} %maximum_bitcast_fusion) | data formatting | bytes 50331648 | tf_op jit(solution)/shard_map/reshape;reshape | solution.py:49
  311.8 12.0 %convolution_convert_fusion = bf16[16,131072]{1,0:T(8,128)(2,1)} fusion(bf16[96,131072]{1,0:T(8,128)(2,1)} %reshape_reshape.3, s32[96]{0:T(128)S(1)} %add.18), kind=kOutput, calls=%fused_computation | convolution fusion | flops 404751872 | bytes 29360512 | tf_op jit(solution)/shard_map/dot_general | solution.py:49
  323.8 5.5 %all_to_all.6 = bf16[8,2,131072]{2,1,0:T(2,128)(2,1)} reshape(bf16[16,131072]{1,0:T(8,128)(2,1)} %convolution_convert_fusion) | data formatting | bytes 8388608 | tf_op jit(solution)/shard_map/all_to_all | solution.py:50
  329.3 6.1 %all-to-all-start = ((bf16[8,2,131072]{2,1,0:T(2,128)(2,1)}), bf16[8,2,131072]{2,1,0:T(2,128)(2,1)}, u32[]{:S(2)}, u32[]{:S(2)}) async-start(bf16[8,2,131072]{2,1,0:T(2,128)(2,1)} %all_to_all.6), calls=%async_computation | async-start | bytes 8388608 | tf_op jit(solution)/shard_map/all_to_all | solution.py:50
  335.4 1.9 pad_maximum_fusion
  337.3 0.0 copy-start.3
  337.3 90.8 %all-to-all-done = bf16[8,2,131072]{2,1,0:T(2,128)(2,1)} async-done(((bf16[8,2,131072]{2,1,0:T(2,128)(2,1)}), bf16[8,2,131072]{2,1,0:T(2,128)(2,1)}, u32[]{:S(2)}, u32[]{:S(2)}) %all-to-all-start) | async-done | bytes 4194336 | tf_op jit(solution)/shard_map/all_to_all | solution.py:50
  428.1 6.3 %convert_reduce_fusion = f32[2,131072]{1,0:T(2,128)S(1)} fusion(bf16[8,2,131072]{2,1,0:T(2,128)(2,1)} %all-to-all-done), kind=kLoop, calls=%fused_computation.5 | loop fusion | flops 3932160 | bytes 5242880 | tf_op jit(solution)/shard_map/reduce_sum | solution.py:53
  434.4 0.1 copy.14
  434.5 0.1 copy.11
  434.6 0.0 copy-done.3
  434.6 1.1 bitcast_subtract_fusion
  (2 shorter events, 0.0 us)
Async XLA Ops:
  7.2 46.3 %all-gather.2.cloned.1.call-start = ((), (), s32[]{:S(2)}) async-start(), calls=%async_computation.1 | async-start | bytes 1966080 | tf_op jit(solution)/shard_map/all_gather | solution.py:19
  7.2 6.2 %collective-permute-start = (bf16[2,6,512,256]{3,2,1,0:T(8,128)(2,1)}, bf16[2,6,512,256]{3,2,1,0:T(8,128)(2,1)}, u32[]{:S(2)}, u32[]{:S(2)}) collective-permute-start(bf16[2,6,512,256]{3,2,1,0:T(8,128)(2,1)} %param.5), channel_id=1, source_target_pairs={{0,8},{8,0},{16,24},{24,16},{1,9},{9,1},{17,25},{25,17},{2,10},{10... | collective-permute-start | bytes 9437192 | tf_op jit(solution)/shard_map/ppermute | solution.py:28
  7.8 17.1 %copy-start.4 = (s32[6,2,8]{2,1,0:T(2,128)S(1)}, s32[6,2,8]{2,1,0:T(2,128)}, u32[]{:S(2)}) copy-start(s32[6,2,8]{2,1,0:T(2,128)} %param.8) | copy-start | bytes 1156
  7.8 17.1 %copy-start.5 = (s32[6,2,8]{2,1,0:T(2,128)S(1)}, s32[6,2,8]{2,1,0:T(2,128)}, u32[]{:S(2)}) copy-start(s32[6,2,8]{2,1,0:T(2,128)} %param.7) | copy-start | bytes 1156
  7.8 45.7 %copy-start = (bf16[2,6,512,256]{3,2,1,0:T(8,128)(2,1)S(1)}, bf16[2,6,512,256]{3,2,1,0:T(8,128)(2,1)}, u32[]{:S(2)}) copy-start(bf16[2,6,512,256]{3,2,1,0:T(8,128)(2,1)} %param.5) | copy-start | bytes 9437188
  22.0 147.4 %collective-permute-start.1 = (bf16[2,6,1024,256]{3,2,1,0:T(8,128)(2,1)}, bf16[2,6,1024,256]{3,2,1,0:T(8,128)(2,1)}, u32[]{:S(2)}, u32[]{:S(2)}) collective-permute-start(bf16[2,6,1024,256]{3,2,1,0:T(8,128)(2,1)} %maximum_select_fusion.1), channel_id=1, source_target_pairs={{0,16},{8,24},{16,0},{24,8},{1,17},{9,25},{17,1},{25,9},{2,18},{10... | collective-permute-start | bytes 18874376 | tf_op jit(solution)/shard_map/ppermute | solution.py:28
  53.5 3.6 copy-start.1
  53.5 3.6 copy-start.2
  260.8 15.8 %slice-start = ((s8[12582912]{0:T(1024)(128)(4,1)}), s8[4194304]{0:T(1024)(128)(4,1)S(1)}, s32[]{:S(2)}) async-start(s8[12582912]{0:T(1024)(128)(4,1)} %bitcast.56), calls=%async_computation.2 | async-start | bytes 8388608
  260.8 15.8 %slice-start.1 = ((s8[12582912]{0:T(1024)(128)(4,1)}), s8[4194304]{0:T(1024)(128)(4,1)S(1)}, s32[]{:S(2)}) async-start(s8[12582912]{0:T(1024)(128)(4,1)} %bitcast.56), calls=%async_computation.3 | async-start | bytes 8388608
  270.5 6.2 %slice-start.2 = ((s8[12582912]{0:T(1024)(128)(4,1)}), s8[4194304]{0:T(1024)(128)(4,1)S(1)}, s32[]{:S(2)}) async-start(s8[12582912]{0:T(1024)(128)(4,1)} %bitcast.56), calls=%async_computation.4 | async-start | bytes 8388608
  329.3 98.8 %all-to-all-start = ((bf16[8,2,131072]{2,1,0:T(2,128)(2,1)}), bf16[8,2,131072]{2,1,0:T(2,128)(2,1)}, u32[]{:S(2)}, u32[]{:S(2)}) async-start(bf16[8,2,131072]{2,1,0:T(2,128)(2,1)} %all_to_all.6), calls=%async_computation | async-start | bytes 8388608 | tf_op jit(solution)/shard_map/all_to_all | solution.py:50
  337.3 97.3 %copy-start.3 = (f32[2,512,256]{2,1,0:T(8,128)S(1)}, f32[2,512,256]{2,1,0:T(8,128)}, u32[]{:S(2)}) copy-start(f32[2,512,256]{2,1,0:T(8,128)} %param.9) | copy-start | bytes 3145732
Sparse Core Ops, SparseCore 0:
  25.0 28.4 all-gather.1
